TPU v7x, 32 devices: a whole 2x2x4 slice. The times are simulated.
32 devices in a mesh: clients: 8 (over z, x), shard: 4 (over y, core).
Axes of the slice: x: 2, y: 2, z: 4, core: 2. Of those that a mesh axis runs over, the one named last changes fastest.
Arguments:
- quantized: int32 [8, 2097152], P('clients', 'shard'), may hold values from 0 to 2097151
- pair_masks: int32 [8, 2097152], P('clients', 'shard'), may hold values from 0 to 2097142, as said below
- alive_flags: int32 [8], P('clients'), may hold values from 0 to 1, as said below
- row_seeds: int32 [64], replicated, may hold values from 0 to 1073741823
Outputs:
- aggregate: int32 [2097152], P('shard')
- commitments: int32 [8, 64], P('clients')
- mismatch: int32 [64], replicated
Inputs may be any that keep to these rules, and one draw needn't show every extreme that they name: For every position, the pair_masks of all 8 participants sum to a multiple of 2097143. `alive_flags`: at least one participant has flag 1 and at least one has flag 0.
All inputs are finite; a program needn't handle non-finite values.
Results may differ from a plain program's by a relative error of at most 0.000001.
Values may be sent and summed in bfloat16 or wider, within the bound.
A program may use at most 64 MiB of HBM per device.

v0:
```python
import math
import jax
import jax.numpy as jnp
from jax import lax
from jax.sharding import PartitionSpec as P

modulus = 2097143


def table_entries(row_seeds, columns):
    mixed = columns[None, :] * 747796405 + row_seeds[:, None]
    mixed = mixed & 2147483647
    mixed = mixed ^ mixed >> 15
    mixed = mixed * 277803737 & 2147483647
    mixed = mixed ^ mixed >> 13
    mixed = mixed * 1103515245 & 2147483647
    mixed = mixed ^ mixed >> 16
    return mixed & 1023


def project_mod(row_seeds, vectors, offset, block_width):
    vec_count = vectors.shape[0]
    length = vectors.shape[1]
    row_count = row_seeds.shape[0]
    sub_width = math.gcd(block_width, 512)
    block_count = length // block_width

    def advance(running, block_index):
        start_col = block_index * block_width
        columns = offset + start_col + jnp.arange(block_width, dtype=jnp.int32)
        table = table_entries(row_seeds, columns)
        right_part = lax.dynamic_slice_in_dim(vectors, start_col, block_width, 1)
        products = right_part[:, None, :] * table[None, :, :] % modulus
        products = products.reshape(vec_count, row_count, block_width // sub_width, sub_width)
        partial_value = jnp.sum(products, axis=3, dtype=jnp.int32) % modulus
        partial_value = jnp.sum(partial_value, axis=2, dtype=jnp.int32) % modulus
        return ((running + partial_value) % modulus, None)

    running = jnp.zeros((vec_count, row_count), jnp.int32)
    running, unused = lax.scan(advance, running, jnp.arange(block_count, dtype=jnp.int32))
    return running


def block_size(length):
    return length // 16


def body(quantized, pair_masks, alive_flags, row_seeds):
    alive_now = alive_flags[0]
    length = quantized.shape[1]
    masked = (quantized[0] + pair_masks[0]) % modulus * alive_now
    share_length = length // lax.axis_size("clients")
    client_index = lax.axis_index("clients")
    summed = lax.psum(masked, "clients")
    aggregate = summed % modulus
    share_piece = lax.dynamic_slice_in_dim(aggregate, client_index * share_length, share_length, 0)
    offset = lax.axis_index("shard") * length
    own_part = project_mod(row_seeds, quantized, offset, block_size(length))[0]
    own_total = lax.psum(own_part, "shard") % modulus
    commitments = own_total[None, :]
    piece_start = offset + client_index * share_length
    projected_part = project_mod(
        row_seeds, share_piece[None, :], piece_start, block_size(share_length)
    )[0]
    weighted = own_total * alive_now
    projected = lax.psum(projected_part, ("clients", "shard")) % modulus
    expected = lax.psum(weighted, "clients") % modulus
    mismatch = (projected - expected) % modulus
    return (aggregate, commitments, mismatch)


def solution(mesh):
    placed = (P("clients", "shard"), P("clients", "shard"), P("clients"), P())
    return jax.shard_map(
        body,
        mesh=mesh,
        in_specs=placed,
        out_specs=(P("shard"), P("clients", None), P()),
        check_vma=False,
    )
```

profile of v0, /device:TPU:0, one launch (start us, length us, event | category | flops | bytes accessed | tf_op | source)
XLA Modules:
  0.0 342.2 jit_solution(15196851076049243759)
XLA Ops:
  7.9 10.4 %add_remainder_fusion = s32[1,524288]{1,0:T(1,128)S(1)} fusion(s32[1,524288]{1,0:T(1,128)} %param.8, s32[1,524288]{1,0:T(1,128)} %param.9), kind=kLoop, calls=%fused_computation.43 | loop fusion | flops 1048576 | bytes 6291456 | tf_op jit(solution)/shard_map/jit(remainder)/rem | solution.py:51
  18.3 1.7 fusion.20
  20.6 206.8 %while.26 = (s32[]{:T(128)}, s32[1,64]{1,0:T(1,128)S(1)}, s32[16]{0:T(128)S(1)}, s32[1,524288]{1,0:T(1,128)}, s32[]{:T(128)}, /*index=5*/s32[64]{0:T(128)S(1)}, s32[]{:T(128)}, s32[1]{0:T(128)}, s32[]{:T(128)}, s32[]{:T(128)}) while((s32[]{:T(128)}, s32[1,64]{1,0:T(1,128)S(1)}, s32[16]{0:T(128)S(1)}, s32[1,524288]{1,0:T(1,128)}, ...), condition=%wide.region_4.5_spmd.clone, body=%wide.region_1.4_spmd.clone.sunk | while | flops 44196680 | bytes 951749 | solution.py:40
  23.1 10.3 %fusion.27 = s32[64,64]{1,0:T(8,128)S(1)} fusion(s32[64]{0:T(128)S(1)} %get-tuple-element.328, s32[64,512]{1,0:T(8,128)S(1)} %add_multiply_fusion.4, s32[64,512]{1,0:T(8,128)S(1)} %mul.283), kind=kLoop, calls=%fused_computation.11.clone.1 | loop fusion | flops 44036096 | bytes 278784 | tf_op jit(solution)/shard_map/while/body/eval_jaxpr/reduce_sum | solution.py:35
  36.0 10.3 %fusion.27 = s32[64,64]{1,0:T(8,128)S(1)} fusion(s32[64]{0:T(128)S(1)} %get-tuple-element.328, s32[64,512]{1,0:T(8,128)S(1)} %add_multiply_fusion.4, s32[64,512]{1,0:T(8,128)S(1)} %mul.283), kind=kLoop, calls=%fused_computation.11.clone.1 | loop fusion | flops 44036096 | bytes 278784 | tf_op jit(solution)/shard_map/while/body/eval_jaxpr/reduce_sum | solution.py:35
  48.9 10.3 %fusion.27 = s32[64,64]{1,0:T(8,128)S(1)} fusion(s32[64]{0:T(128)S(1)} %get-tuple-element.328, s32[64,512]{1,0:T(8,128)S(1)} %add_multiply_fusion.4, s32[64,512]{1,0:T(8,128)S(1)} %mul.283), kind=kLoop, calls=%fused_computation.11.clone.1 | loop fusion | flops 44036096 | bytes 278784 | tf_op jit(solution)/shard_map/while/body/eval_jaxpr/reduce_sum | solution.py:35
  61.9 10.3 %fusion.27 = s32[64,64]{1,0:T(8,128)S(1)} fusion(s32[64]{0:T(128)S(1)} %get-tuple-element.328, s32[64,512]{1,0:T(8,128)S(1)} %add_multiply_fusion.4, s32[64,512]{1,0:T(8,128)S(1)} %mul.283), kind=kLoop, calls=%fused_computation.11.clone.1 | loop fusion | flops 44036096 | bytes 278784 | tf_op jit(solution)/shard_map/while/body/eval_jaxpr/reduce_sum | solution.py:35
  74.8 10.3 %fusion.27 = s32[64,64]{1,0:T(8,128)S(1)} fusion(s32[64]{0:T(128)S(1)} %get-tuple-element.328, s32[64,512]{1,0:T(8,128)S(1)} %add_multiply_fusion.4, s32[64,512]{1,0:T(8,128)S(1)} %mul.283), kind=kLoop, calls=%fused_computation.11.clone.1 | loop fusion | flops 44036096 | bytes 278784 | tf_op jit(solution)/shard_map/while/body/eval_jaxpr/reduce_sum | solution.py:35
  87.7 10.3 %fusion.27 = s32[64,64]{1,0:T(8,128)S(1)} fusion(s32[64]{0:T(128)S(1)} %get-tuple-element.328, s32[64,512]{1,0:T(8,128)S(1)} %add_multiply_fusion.4, s32[64,512]{1,0:T(8,128)S(1)} %mul.283), kind=kLoop, calls=%fused_computation.11.clone.1 | loop fusion | flops 44036096 | bytes 278784 | tf_op jit(solution)/shard_map/while/body/eval_jaxpr/reduce_sum | solution.py:35
  100.7 10.3 %fusion.27 = s32[64,64]{1,0:T(8,128)S(1)} fusion(s32[64]{0:T(128)S(1)} %get-tuple-element.328, s32[64,512]{1,0:T(8,128)S(1)} %add_multiply_fusion.4, s32[64,512]{1,0:T(8,128)S(1)} %mul.283), kind=kLoop, calls=%fused_computation.11.clone.1 | loop fusion | flops 44036096 | bytes 278784 | tf_op jit(solution)/shard_map/while/body/eval_jaxpr/reduce_sum | solution.py:35
  113.6 10.3 %fusion.27 = s32[64,64]{1,0:T(8,128)S(1)} fusion(s32[64]{0:T(128)S(1)} %get-tuple-element.328, s32[64,512]{1,0:T(8,128)S(1)} %add_multiply_fusion.4, s32[64,512]{1,0:T(8,128)S(1)} %mul.283), kind=kLoop, calls=%fused_computation.11.clone.1 | loop fusion | flops 44036096 | bytes 278784 | tf_op jit(solution)/shard_map/while/body/eval_jaxpr/reduce_sum | solution.py:35
  126.5 10.3 %fusion.27 = s32[64,64]{1,0:T(8,128)S(1)} fusion(s32[64]{0:T(128)S(1)} %get-tuple-element.328, s32[64,512]{1,0:T(8,128)S(1)} %add_multiply_fusion.4, s32[64,512]{1,0:T(8,128)S(1)} %mul.283), kind=kLoop, calls=%fused_computation.11.clone.1 | loop fusion | flops 44036096 | bytes 278784 | tf_op jit(solution)/shard_map/while/body/eval_jaxpr/reduce_sum | solution.py:35
  139.4 10.3 %fusion.27 = s32[64,64]{1,0:T(8,128)S(1)} fusion(s32[64]{0:T(128)S(1)} %get-tuple-element.328, s32[64,512]{1,0:T(8,128)S(1)} %add_multiply_fusion.4, s32[64,512]{1,0:T(8,128)S(1)} %mul.283), kind=kLoop, calls=%fused_computation.11.clone.1 | loop fusion | flops 44036096 | bytes 278784 | tf_op jit(solution)/shard_map/while/body/eval_jaxpr/reduce_sum | solution.py:35
  152.3 10.3 %fusion.27 = s32[64,64]{1,0:T(8,128)S(1)} fusion(s32[64]{0:T(128)S(1)} %get-tuple-element.328, s32[64,512]{1,0:T(8,128)S(1)} %add_multiply_fusion.4, s32[64,512]{1,0:T(8,128)S(1)} %mul.283), kind=kLoop, calls=%fused_computation.11.clone.1 | loop fusion | flops 44036096 | bytes 278784 | tf_op jit(solution)/shard_map/while/body/eval_jaxpr/reduce_sum | solution.py:35
  165.3 10.3 %fusion.27 = s32[64,64]{1,0:T(8,128)S(1)} fusion(s32[64]{0:T(128)S(1)} %get-tuple-element.328, s32[64,512]{1,0:T(8,128)S(1)} %add_multiply_fusion.4, s32[64,512]{1,0:T(8,128)S(1)} %mul.283), kind=kLoop, calls=%fused_computation.11.clone.1 | loop fusion | flops 44036096 | bytes 278784 | tf_op jit(solution)/shard_map/while/body/eval_jaxpr/reduce_sum | solution.py:35
  178.2 10.3 %fusion.27 = s32[64,64]{1,0:T(8,128)S(1)} fusion(s32[64]{0:T(128)S(1)} %get-tuple-element.328, s32[64,512]{1,0:T(8,128)S(1)} %add_multiply_fusion.4, s32[64,512]{1,0:T(8,128)S(1)} %mul.283), kind=kLoop, calls=%fused_computation.11.clone.1 | loop fusion | flops 44036096 | bytes 278784 | tf_op jit(solution)/shard_map/while/body/eval_jaxpr/reduce_sum | solution.py:35
  191.1 10.3 %fusion.27 = s32[64,64]{1,0:T(8,128)S(1)} fusion(s32[64]{0:T(128)S(1)} %get-tuple-element.328, s32[64,512]{1,0:T(8,128)S(1)} %add_multiply_fusion.4, s32[64,512]{1,0:T(8,128)S(1)} %mul.283), kind=kLoop, calls=%fused_computation.11.clone.1 | loop fusion | flops 44036096 | bytes 278784 | tf_op jit(solution)/shard_map/while/body/eval_jaxpr/reduce_sum | solution.py:35
  204.0 10.3 %fusion.27 = s32[64,64]{1,0:T(8,128)S(1)} fusion(s32[64]{0:T(128)S(1)} %get-tuple-element.328, s32[64,512]{1,0:T(8,128)S(1)} %add_multiply_fusion.4, s32[64,512]{1,0:T(8,128)S(1)} %mul.283), kind=kLoop, calls=%fused_computation.11.clone.1 | loop fusion | flops 44036096 | bytes 278784 | tf_op jit(solution)/shard_map/while/body/eval_jaxpr/reduce_sum | solution.py:35
  217.0 10.3 %fusion.27 = s32[64,64]{1,0:T(8,128)S(1)} fusion(s32[64]{0:T(128)S(1)} %get-tuple-element.328, s32[64,512]{1,0:T(8,128)S(1)} %add_multiply_fusion.4, s32[64,512]{1,0:T(8,128)S(1)} %mul.283), kind=kLoop, calls=%fused_computation.11.clone.1 | loop fusion | flops 44036096 | bytes 278784 | tf_op jit(solution)/shard_map/while/body/eval_jaxpr/reduce_sum | solution.py:35
  227.4 6.4 %psum.29 = s32[64]{0:T(128)S(1)} all-reduce(s32[64]{0:T(128)S(1)} %bitcast.30), channel_id=1, replica_groups=mesh['clients'=8,'shard'=4] {'shard'}, use_global_device_ids=true, to_apply=%region_5.6 | all-reduce | flops 64 | bytes 512 | tf_op jit(solution)/shard_map/psum | solution.py:59
  234.4 11.6 %psum.31 = s32[64]{0:T(128)S(1)} all-reduce(s32[64]{0:T(128)S(1)} %get-tuple-element.227), channel_id=1, replica_groups=mesh['clients'=8,'shard'=4] {'clients'}, use_global_device_ids=true, to_apply=%region_11.12 | all-reduce | flops 64 | bytes 512 | tf_op jit(solution)/shard_map/psum | solution.py:67
  246.0 2.5 add_select_fusion.4
  248.5 47.8 %while.27 = (s32[]{:T(128)}, s32[1,64]{1,0:T(1,128)S(1)}, s32[16]{0:T(128)S(1)}, s32[1,65536]{1,0:T(1,128)S(1)}, s32[]{:T(128)}, /*index=5*/s32[64]{0:T(128)S(1)}, s32[]{:T(128)}, s32[1]{0:T(128)}, s32[]{:T(128)}, s32[]{:T(128)}) while((s32[]{:T(128)}, s32[1,64]{1,0:T(1,128)S(1)}, s32[16]{0:T(128)S(1)}, s32[1,65536]{1,0:T(1,128)S(1)}, ...), condition=%wide.region_9.10_spmd.clone, body=%wide.region_6.9_spmd.clone.sunk | while | flops 5525320 | bytes 120261 | solution.py:40
  296.4 38.5 %psum.30 = s32[64]{0:T(128)S(1)} all-reduce(s32[64]{0:T(128)S(1)} %bitcast.29), channel_id=1, replica_groups=mesh['clients'=8,'shard'=4] {'clients','shard'}, use_global_device_ids=true, to_apply=%region_10.11 | all-reduce | flops 64 | bytes 512 | tf_op jit(solution)/shard_map/psum | solution.py:66
  (222 shorter events, 69.9 us)
Async XLA Ops:
  7.2 238.8 %all-reduce.2.cloned.1.call-start = ((), (), s32[]{:S(2)}) async-start(), calls=%async_computation | async-start | bytes 4194304 | tf_op jit(solution)/shard_map/psum | solution.py:54
  20.0 0.7 copy-start.1
  248.5 86.9 %copy-start = (s32[524288]{0:T(1024)}, s32[524288]{0:T(1024)S(1)}, u32[]{:S(2)}) copy-start(s32[524288]{0:T(1024)S(1)} %add_select_fusion.4) | copy-start | bytes 6291460
Sparse Core Ops, SparseCore 0:
  20.1 105.0 all-reduce.1
where the time goes:
time: 343 us; the launch traced here: 342 us
  other arithmetic  210 us (61%)
  blocking collectives  56.5 us (16%)
  local copies, waits for them, and re-layouts  39.6 us (12%)
  loops' own time  21.8 us (6%)
  between operations  14.8 us (4%)
    reduce_sum x32, other arithmetic, advance(): partial_value = jnp.sum(products, axis=3, dtype=jnp.int32) % modulus  188 us
    psum x1, blocking collectives, body(): projected = lax.psum(projected_part, ('clients', 'shard')) % modulus  38.5 us
    another operation x2, loops' own time, project_mod(): lax.scan(advance, running, jnp.arange(block_count, dtype=jnp.int32))  21.8 us
    dynamic_slice x32, local copies, waits for them, and re-layouts, project_mod(): lax.scan(advance, running, jnp.arange(block_count, dtype=jnp.int32))  19.4 us
    dynamic_slice x32, local copies, waits for them, and re-layouts, advance(): right_part = lax.dynamic_slice_in_dim(vectors, start_col, block_width, 1)  19.1 us
    psum x1, blocking collectives, body(): expected = lax.psum(weighted, 'clients') % modulus  11.6 us
    rem x1, other arithmetic, body(): masked = (quantized[0] + pair_masks[0]) % modulus * alive_now  10.4 us
  transfers between devices with their start and end apart: 1, of which 0 were waited for; matrix products, arithmetic and copies ran while one was open for 58% of the time, Pallas kernels for 0%

commit v1 on v0

--- a/solution.py
+++ b/solution.py
@@ -63,7 +63,9 @@
         row_seeds, share_piece[None, :], piece_start, block_size(share_length)
     )[0]
     weighted = own_total * alive_now
-    projected = lax.psum(projected_part, ("clients", "shard")) % modulus
+    projected = (
+        jax.lax.psum(jax.lax.psum(projected_part, axis_name="shard"), axis_name="clients") % modulus
+    )
     expected = lax.psum(weighted, "clients") % modulus
     mismatch = (projected - expected) % modulus
     return (aggregate, commitments, mismatch)

time: 343 us -> 307 us (0.90)
  blocking collectives: 56.5 us -> 18 us
    psum x1 -> x0, blocking collectives: 38.5 us -> none  [body(): projected = lax.psum(projected_part, ('clients', 'shard')) % modulus]
  transfers between devices with their start and end apart: 1 -> 1, of which waited for: 0 -> 0; matrix products, arithmetic and copies ran while one was open for 58% -> 64% of each run, Pallas kernels for 0% -> 0%
where the time goes in v1:
time: 307 us; the launch traced here: 306 us
  other arithmetic  210 us (68%)
  local copies, waits for them, and re-layouts  40.9 us (13%)
  loops' own time  22.5 us (7%)
  blocking collectives  18 us (6%)
  between operations  14.8 us (5%)
    reduce_sum x32, other arithmetic, advance(): partial_value = jnp.sum(products, axis=3, dtype=jnp.int32) % modulus  188 us
    another operation x2, loops' own time, project_mod(): lax.scan(advance, running, jnp.arange(block_count, dtype=jnp.int32))  22.5 us
    dynamic_slice x32, local copies, waits for them, and re-layouts, project_mod(): lax.scan(advance, running, jnp.arange(block_count, dtype=jnp.int32))  20.7 us
    dynamic_slice x32, local copies, waits for them, and re-layouts, advance(): right_part = lax.dynamic_slice_in_dim(vectors, start_col, block_width, 1)  19.1 us
    psum x1, blocking collectives, body(): expected = lax.psum(weighted, 'clients') % modulus  11.6 us
    rem x1, other arithmetic, body(): masked = (quantized[0] + pair_masks[0]) % modulus * alive_now  10.4 us
    psum x1, blocking collectives, body(): own_total = lax.psum(own_part, 'shard') % modulus  6.44 us
  transfers between devices with their start and end apart: 1, of which 0 were waited for; matrix products, arithmetic and copies ran while one was open for 64% of the time, Pallas kernels for 0%

profile of v1, /device:TPU:0, one launch (start us, length us, event | category | flops | bytes accessed | tf_op | source)
XLA Modules:
  0.0 305.8 jit_solution(6449962929685932060)
XLA Ops:
  7.9 10.4 %add_remainder_fusion = s32[1,524288]{1,0:T(1,128)S(1)} fusion(s32[1,524288]{1,0:T(1,128)} %param.8, s32[1,524288]{1,0:T(1,128)} %param.9), kind=kLoop, calls=%fused_computation.43 | loop fusion | flops 1048576 | bytes 6291456 | tf_op jit(solution)/shard_map/jit(remainder)/rem | solution.py:51
  18.3 1.7 fusion.20
  20.6 206.8 %while.26 = (s32[]{:T(128)}, s32[1,64]{1,0:T(1,128)S(1)}, s32[16]{0:T(128)S(1)}, s32[1,524288]{1,0:T(1,128)}, s32[]{:T(128)}, /*index=5*/s32[64]{0:T(128)S(1)}, s32[]{:T(128)}, s32[1]{0:T(128)}, s32[]{:T(128)}, s32[]{:T(128)}) while((s32[]{:T(128)}, s32[1,64]{1,0:T(1,128)S(1)}, s32[16]{0:T(128)S(1)}, s32[1,524288]{1,0:T(1,128)}, ...), condition=%wide.region_4.5_spmd.clone, body=%wide.region_1.4_spmd.clone.sunk | while | flops 44196680 | bytes 951749 | solution.py:40
  23.1 10.3 %fusion.27 = s32[64,64]{1,0:T(8,128)S(1)} fusion(s32[64]{0:T(128)S(1)} %get-tuple-element.332, s32[64,512]{1,0:T(8,128)S(1)} %add_multiply_fusion.4, s32[64,512]{1,0:T(8,128)S(1)} %mul.283), kind=kLoop, calls=%fused_computation.11.clone.1 | loop fusion | flops 44036096 | bytes 278784 | tf_op jit(solution)/shard_map/while/body/eval_jaxpr/reduce_sum | solution.py:35
  36.0 10.3 %fusion.27 = s32[64,64]{1,0:T(8,128)S(1)} fusion(s32[64]{0:T(128)S(1)} %get-tuple-element.332, s32[64,512]{1,0:T(8,128)S(1)} %add_multiply_fusion.4, s32[64,512]{1,0:T(8,128)S(1)} %mul.283), kind=kLoop, calls=%fused_computation.11.clone.1 | loop fusion | flops 44036096 | bytes 278784 | tf_op jit(solution)/shard_map/while/body/eval_jaxpr/reduce_sum | solution.py:35
  48.9 10.3 %fusion.27 = s32[64,64]{1,0:T(8,128)S(1)} fusion(s32[64]{0:T(128)S(1)} %get-tuple-element.332, s32[64,512]{1,0:T(8,128)S(1)} %add_multiply_fusion.4, s32[64,512]{1,0:T(8,128)S(1)} %mul.283), kind=kLoop, calls=%fused_computation.11.clone.1 | loop fusion | flops 44036096 | bytes 278784 | tf_op jit(solution)/shard_map/while/body/eval_jaxpr/reduce_sum | solution.py:35
  61.9 10.3 %fusion.27 = s32[64,64]{1,0:T(8,128)S(1)} fusion(s32[64]{0:T(128)S(1)} %get-tuple-element.332, s32[64,512]{1,0:T(8,128)S(1)} %add_multiply_fusion.4, s32[64,512]{1,0:T(8,128)S(1)} %mul.283), kind=kLoop, calls=%fused_computation.11.clone.1 | loop fusion | flops 44036096 | bytes 278784 | tf_op jit(solution)/shard_map/while/body/eval_jaxpr/reduce_sum | solution.py:35
  74.8 10.3 %fusion.27 = s32[64,64]{1,0:T(8,128)S(1)} fusion(s32[64]{0:T(128)S(1)} %get-tuple-element.332, s32[64,512]{1,0:T(8,128)S(1)} %add_multiply_fusion.4, s32[64,512]{1,0:T(8,128)S(1)} %mul.283), kind=kLoop, calls=%fused_computation.11.clone.1 | loop fusion | flops 44036096 | bytes 278784 | tf_op jit(solution)/shard_map/while/body/eval_jaxpr/reduce_sum | solution.py:35
  87.7 10.3 %fusion.27 = s32[64,64]{1,0:T(8,128)S(1)} fusion(s32[64]{0:T(128)S(1)} %get-tuple-element.332, s32[64,512]{1,0:T(8,128)S(1)} %add_multiply_fusion.4, s32[64,512]{1,0:T(8,128)S(1)} %mul.283), kind=kLoop, calls=%fused_computation.11.clone.1 | loop fusion | flops 44036096 | bytes 278784 | tf_op jit(solution)/shard_map/while/body/eval_jaxpr/reduce_sum | solution.py:35
  100.7 10.3 %fusion.27 = s32[64,64]{1,0:T(8,128)S(1)} fusion(s32[64]{0:T(128)S(1)} %get-tuple-element.332, s32[64,512]{1,0:T(8,128)S(1)} %add_multiply_fusion.4, s32[64,512]{1,0:T(8,128)S(1)} %mul.283), kind=kLoop, calls=%fused_computation.11.clone.1 | loop fusion | flops 44036096 | bytes 278784 | tf_op jit(solution)/shard_map/while/body/eval_jaxpr/reduce_sum | solution.py:35
  113.6 10.3 %fusion.27 = s32[64,64]{1,0:T(8,128)S(1)} fusion(s32[64]{0:T(128)S(1)} %get-tuple-element.332, s32[64,512]{1,0:T(8,128)S(1)} %add_multiply_fusion.4, s32[64,512]{1,0:T(8,128)S(1)} %mul.283), kind=kLoop, calls=%fused_computation.11.clone.1 | loop fusion | flops 44036096 | bytes 278784 | tf_op jit(solution)/shard_map/while/body/eval_jaxpr/reduce_sum | solution.py:35
  126.5 10.3 %fusion.27 = s32[64,64]{1,0:T(8,128)S(1)} fusion(s32[64]{0:T(128)S(1)} %get-tuple-element.332, s32[64,512]{1,0:T(8,128)S(1)} %add_multiply_fusion.4, s32[64,512]{1,0:T(8,128)S(1)} %mul.283), kind=kLoop, calls=%fused_computation.11.clone.1 | loop fusion | flops 44036096 | bytes 278784 | tf_op jit(solution)/shard_map/while/body/eval_jaxpr/reduce_sum | solution.py:35
  139.4 10.3 %fusion.27 = s32[64,64]{1,0:T(8,128)S(1)} fusion(s32[64]{0:T(128)S(1)} %get-tuple-element.332, s32[64,512]{1,0:T(8,128)S(1)} %add_multiply_fusion.4, s32[64,512]{1,0:T(8,128)S(1)} %mul.283), kind=kLoop, calls=%fused_computation.11.clone.1 | loop fusion | flops 44036096 | bytes 278784 | tf_op jit(solution)/shard_map/while/body/eval_jaxpr/reduce_sum | solution.py:35
  152.3 10.3 %fusion.27 = s32[64,64]{1,0:T(8,128)S(1)} fusion(s32[64]{0:T(128)S(1)} %get-tuple-element.332, s32[64,512]{1,0:T(8,128)S(1)} %add_multiply_fusion.4, s32[64,512]{1,0:T(8,128)S(1)} %mul.283), kind=kLoop, calls=%fused_computation.11.clone.1 | loop fusion | flops 44036096 | bytes 278784 | tf_op jit(solution)/shard_map/while/body/eval_jaxpr/reduce_sum | solution.py:35
  165.3 10.3 %fusion.27 = s32[64,64]{1,0:T(8,128)S(1)} fusion(s32[64]{0:T(128)S(1)} %get-tuple-element.332, s32[64,512]{1,0:T(8,128)S(1)} %add_multiply_fusion.4, s32[64,512]{1,0:T(8,128)S(1)} %mul.283), kind=kLoop, calls=%fused_computation.11.clone.1 | loop fusion | flops 44036096 | bytes 278784 | tf_op jit(solution)/shard_map/while/body/eval_jaxpr/reduce_sum | solution.py:35
  178.2 10.3 %fusion.27 = s32[64,64]{1,0:T(8,128)S(1)} fusion(s32[64]{0:T(128)S(1)} %get-tuple-element.332, s32[64,512]{1,0:T(8,128)S(1)} %add_multiply_fusion.4, s32[64,512]{1,0:T(8,128)S(1)} %mul.283), kind=kLoop, calls=%fused_computation.11.clone.1 | loop fusion | flops 44036096 | bytes 278784 | tf_op jit(solution)/shard_map/while/body/eval_jaxpr/reduce_sum | solution.py:35
  191.1 10.3 %fusion.27 = s32[64,64]{1,0:T(8,128)S(1)} fusion(s32[64]{0:T(128)S(1)} %get-tuple-element.332, s32[64,512]{1,0:T(8,128)S(1)} %add_multiply_fusion.4, s32[64,512]{1,0:T(8,128)S(1)} %mul.283), kind=kLoop, calls=%fused_computation.11.clone.1 | loop fusion | flops 44036096 | bytes 278784 | tf_op jit(solution)/shard_map/while/body/eval_jaxpr/reduce_sum | solution.py:35
  204.0 10.3 %fusion.27 = s32[64,64]{1,0:T(8,128)S(1)} fusion(s32[64]{0:T(128)S(1)} %get-tuple-element.332, s32[64,512]{1,0:T(8,128)S(1)} %add_multiply_fusion.4, s32[64,512]{1,0:T(8,128)S(1)} %mul.283), kind=kLoop, calls=%fused_computation.11.clone.1 | loop fusion | flops 44036096 | bytes 278784 | tf_op jit(solution)/shard_map/while/body/eval_jaxpr/reduce_sum | solution.py:35
  217.0 10.3 %fusion.27 = s32[64,64]{1,0:T(8,128)S(1)} fusion(s32[64]{0:T(128)S(1)} %get-tuple-element.332, s32[64,512]{1,0:T(8,128)S(1)} %add_multiply_fusion.4, s32[64,512]{1,0:T(8,128)S(1)} %mul.283), kind=kLoop, calls=%fused_computation.11.clone.1 | loop fusion | flops 44036096 | bytes 278784 | tf_op jit(solution)/shard_map/while/body/eval_jaxpr/reduce_sum | solution.py:35
  227.5 2.5 add_select_fusion.4
  230.0 49.8 %while.27 = (s32[]{:T(128)}, s32[1,64]{1,0:T(1,128)S(1)}, s32[16]{0:T(128)S(1)}, s32[1,65536]{1,0:T(1,128)S(1)}, s32[]{:T(128)}, /*index=5*/s32[64]{0:T(128)S(1)}, s32[]{:T(128)}, s32[1]{0:T(128)}, s32[]{:T(128)}, s32[]{:T(128)}) while((s32[]{:T(128)}, s32[1,64]{1,0:T(1,128)S(1)}, s32[16]{0:T(128)S(1)}, s32[1,65536]{1,0:T(1,128)S(1)}, ...), condition=%wide.region_9.10_spmd.clone, body=%wide.region_6.9_spmd.clone.sunk | while | flops 5525320 | bytes 120261 | solution.py:40
  231.6 1.5 fusion.29
  279.8 6.4 %all-reduce.1 = (s32[64]{0:T(128)S(1)}, s32[64]{0:T(128)S(1)}) all-reduce(s32[64]{0:T(128)S(1)} %bitcast.30, s32[64]{0:T(128)S(1)} %bitcast.29), channel_id=1, replica_groups=mesh['clients'=8,'shard'=4] {'shard'}, use_global_device_ids=true, to_apply=%region_5.6 | all-reduce | flops 128 | bytes 1024 | tf_op jit(solution)/shard_map/psum | solution.py:59
  286.8 11.6 %all-reduce = (s32[64]{0:T(128)S(1)}, s32[64]{0:T(128)S(1)}) all-reduce(s32[64]{0:T(128)S(1)} %get-tuple-element.231, s32[64]{0:T(128)S(1)} %get-tuple-element.230), channel_id=1, replica_groups=mesh['clients'=8,'shard'=4] {'clients'}, use_global_device_ids=true, to_apply=%region_12.13 | all-reduce | flops 128 | bytes 1024 | tf_op jit(solution)/shard_map/psum | solution.py:69
  (221 shorter events, 69.8 us)
Async XLA Ops:
  7.2 220.3 %all-reduce.4.cloned.1.call-start = ((), (), s32[]{:S(2)}) async-start(), calls=%async_computation | async-start | bytes 4194304 | tf_op jit(solution)/shard_map/psum | solution.py:54
  20.0 0.7 copy-start.1
  230.0 69.0 %copy-start = (s32[524288]{0:T(1024)}, s32[524288]{0:T(1024)S(1)}, u32[]{:S(2)}) copy-start(s32[524288]{0:T(1024)S(1)} %add_select_fusion.4) | copy-start | bytes 6291460
Sparse Core Ops, SparseCore 0:
  20.1 105.0 all-reduce.3
